TPU v7x, 32 devices: a whole 2x2x4 slice. The times are simulated.
32 devices in a mesh: gx: 2 (over x), gy: 16 (over z, y, core).
Axes of the slice: x: 2, y: 2, z: 4, core: 2. Of those that a mesh axis runs over, the one named last changes fastest.
Arguments:
- cell: int32 [1048576], P(('gx', 'gy')), may hold values from 0 to 524287
- vehicle: int32 [1048576], P(('gx', 'gy')), may hold values from 0 to 1023
- speed: float32 [1048576], P(('gx', 'gy')), may hold values from 0 to 64, as said below
Outputs:
- top_speed: float32 [524288], P(('gx', 'gy'))
- top_vehicle: int32 [524288], P(('gx', 'gy'))
Inputs may be any that keep to these rules, and one draw needn't show every extreme that they name: Every speed is a whole multiple of 1/1024.
All inputs are finite; a program needn't handle non-finite values.
Results may differ from a plain program's by a relative error of at most 0.0003.
Values sent between devices are 32-bit elements; how exact they have to be, the bound alone decides.
A program may use at most 64 MiB of HBM per device.

v0:
```python
import jax
import jax.numpy as jnp
from jax import lax
from jax.sharding import PartitionSpec as P

CELLS = 524288
VEHICLES = 1024


def swapped(block, axis, apart):
    count = lax.axis_size(axis)
    route = []
    for low in range(count):
        high = low | 1 << apart
        if high != low and high < count:
            route += [(low, high), (high, low)]
    return lax.ppermute(block, axis, route)


def combine(first, second):
    speed_a = first[0]
    speed_b = second[0]
    best = jnp.maximum(speed_a, speed_b)
    ident = jnp.where(
        speed_a > speed_b,
        first[1],
        jnp.where(speed_b > speed_a, second[1], jnp.minimum(first[1], second[1])),
    )
    return jnp.stack([best, ident])


def per_device(cell, vehicle, speed):
    local_best = jnp.full((CELLS,), -1.0, jnp.float32).at[cell].max(speed)
    chosen = jnp.where(speed == local_best[cell], vehicle, VEHICLES)
    local_ident = jnp.full((CELLS,), VEHICLES, jnp.int32).at[cell].min(chosen)
    paired = jnp.stack([local_best, local_ident.astype(jnp.float32)])
    outer = lax.axis_size("gx")
    inner = lax.axis_size("gy")
    nbits = (outer * inner).bit_length() - 1
    myself = lax.axis_index(("gx", "gy"))
    buffer = paired
    for level in reversed(range(nbits)):
        half = buffer.shape[1] // 2
        side = myself >> level & 1
        keep = lax.dynamic_slice_in_dim(buffer, side * half, half, 1)
        give = lax.dynamic_slice_in_dim(buffer, (1 - side) * half, half, 1)
        partner = swapped(give, ("gx", "gy"), level)
        buffer = combine(keep, partner)
    best = buffer[0]
    ident = buffer[1]
    lowest = ident.astype(jnp.int32)
    top_vehicle = jnp.where(lowest < VEHICLES, lowest, -1)
    return (best, top_vehicle)


def solution(mesh):
    placed = (P(("gx", "gy")), P(("gx", "gy")), P(("gx", "gy")))
    return jax.shard_map(
        per_device,
        mesh=mesh,
        in_specs=placed,
        out_specs=(P(("gx", "gy")), P(("gx", "gy"))),
        check_vma=False,
    )
```

profile of v0, /device:TPU:0, one launch (start us, length us, event | category | flops | bytes accessed | tf_op | source)
XLA Modules:
  0.0 671.6 jit_solution(18166627678722901278)
XLA Ops:
  0.6 0.9 broadcast_clamp_fusion
  1.6 171.8 %scatter_custom_fusion = f32[524288]{0:T(1024)S(1)} fusion(s32[32768]{0:T(1024)S(1)} %get-tuple-element.26, f32[32768]{0:T(1024)} %param.5, f32[]{:T(128)} %constant.18.clone.1), kind=kCustom, calls=%fused_computation.25 | custom fusion | flops 32768 | bytes 2097664 | tf_op jit(solution)/shard_map/scatter-max | solution.py:33
  173.5 180.5 %gather_fusion = f32[32768]{0:T(1024)S(1)} fusion(f32[524288]{0:T(1024)S(1)} %scatter_custom_fusion, s32[32768]{0:T(1024)S(1)} %get-tuple-element.25), kind=kCustom, calls=%fused_computation | custom fusion | bytes 393216 | tf_op jit(solution)/shard_map/gather | solution.py:34
  354.1 176.3 %scatter_custom_fusion.1 = s32[524288]{0:T(1024)} fusion(s32[32768]{0:T(1024)S(1)} %get-tuple-element.26, s32[32768]{0:T(1024)S(1)} %compare_select_fusion.10, s32[]{:T(128)} %constant.21.clone.1), kind=kCustom, calls=%fused_computation.23 | custom fusion | flops 32768 | bytes 2097156 | tf_op jit(solution)/shard_map/scatter-min | solution.py:35
  530.4 3.1 convert_element_type.6
  533.5 7.0 %fusion.1 = (f32[2,262144]{1,0:T(2,128)}, f32[2,262144]{1,0:T(2,128)}) fusion(s32[]{:T(128)S(6)} %select_n.88, f32[1,524288]{1,0:T(1,128)S(1)} %bitcast.5, f32[1,524288]{1,0:T(1,128)} %bitcast.6, s32[]{:T(128)S(6)} %select_n.89), kind=kLoop, calls=%fused_computation.14 | loop fusion | flops 1048576 | bytes 8388616 | tf_op jit(solution)/shard_map/stack | solution.py:36
  540.5 3.0 collective-permute-start
  543.5 45.8 %collective-permute-done = f32[2,262144]{1,0:T(2,128)S(1)} collective-permute-done((f32[2,262144]{1,0:T(2,128)}, f32[2,262144]{1,0:T(2,128)S(1)}, u32[]{:S(2)}, u32[]{:S(2)}) %collective-permute-start) | collective-permute-done | bytes 2097184 | tf_op jit(solution)/shard_map/ppermute | solution.py:17
  589.3 4.9 compare_select_fusion.1
  594.2 2.2 fusion.3
  596.5 2.9 collective-permute-start.1
  599.4 44.9 %collective-permute-done.1 = f32[2,131072]{1,0:T(2,128)S(1)} collective-permute-done((f32[2,131072]{1,0:T(2,128)S(1)}, f32[2,131072]{1,0:T(2,128)S(1)}, u32[]{:S(2)}, u32[]{:S(2)}) %collective-permute-start.1) | collective-permute-done | bytes 1048608 | tf_op jit(solution)/shard_map/ppermute | solution.py:17
  644.2 1.4 compare_select_fusion.3
  645.6 1.2 fusion.9
  646.8 0.7 collective-permute-start.2
  647.5 12.2 %collective-permute-done.2 = f32[2,65536]{1,0:T(2,128)S(1)} collective-permute-done((f32[2,65536]{1,0:T(2,128)S(1)}, f32[2,65536]{1,0:T(2,128)S(1)}, u32[]{:S(2)}, u32[]{:S(2)}) %collective-permute-start.2) | collective-permute-done | bytes 524320 | tf_op jit(solution)/shard_map/ppermute | solution.py:17
  659.7 0.7 compare_select_fusion.5
  660.4 0.6 fusion.11
  661.0 1.5 collective-permute-start.3
  662.5 5.1 collective-permute-done.3
  668.4 1.3 collective-permute-done.4
  669.7 0.4 compare_reduce_fusion
  670.1 0.8 fusion.16
  670.9 0.7 compare_select_fusion.9
  (8 shorter events, 0.8 us)
Async XLA Ops:
  173.4 180.6 %copy-start = (f32[32768]{0:T(1024)S(1)}, f32[32768]{0:T(1024)}, u32[]{:S(2)}) copy-start(f32[32768]{0:T(1024)} %param.5) | copy-start | bytes 393220
  173.4 180.6 %copy-start.1 = (s32[32768]{0:T(1024)S(1)}, s32[32768]{0:T(1024)}, u32[]{:S(2)}) copy-start(s32[32768]{0:T(1024)} %param.4) | copy-start | bytes 393220
  540.5 48.8 %collective-permute-start = (f32[2,262144]{1,0:T(2,128)}, f32[2,262144]{1,0:T(2,128)S(1)}, u32[]{:S(2)}, u32[]{:S(2)}) collective-permute-start(f32[2,262144]{1,0:T(2,128)} %get-tuple-element.7), channel_id=1, source_target_pairs={{0,16},{16,0},{1,17},{17,1},{2,18},{18,2},{3,19},{19,3},{4,20},{20... | collective-permute-start | bytes 6291464 | tf_op jit(solution)/shard_map/ppermute | solution.py:17
  596.5 47.8 %collective-permute-start.1 = (f32[2,131072]{1,0:T(2,128)S(1)}, f32[2,131072]{1,0:T(2,128)S(1)}, u32[]{:S(2)}, u32[]{:S(2)}) collective-permute-start(f32[2,131072]{1,0:T(2,128)S(1)} %get-tuple-element.11), channel_id=1, source_target_pairs={{0,8},{8,0},{1,9},{9,1},{2,10},{10,2},{3,11},{11,3},{4,12},{12,4},... | collective-permute-start | bytes 3145736 | tf_op jit(solution)/shard_map/ppermute | solution.py:17
  646.8 12.9 %collective-permute-start.2 = (f32[2,65536]{1,0:T(2,128)S(1)}, f32[2,65536]{1,0:T(2,128)S(1)}, u32[]{:S(2)}, u32[]{:S(2)}) collective-permute-start(f32[2,65536]{1,0:T(2,128)S(1)} %get-tuple-element.15), channel_id=1, source_target_pairs={{0,4},{4,0},{1,5},{5,1},{2,6},{6,2},{3,7},{7,3},{8,12},{12,8},{9,1... | collective-permute-start | bytes 1572872 | tf_op jit(solution)/shard_map/ppermute | solution.py:17
  661.0 6.6 collective-permute-start.3
  668.3 1.4 collective-permute-start.4
where the time goes:
time: 672 us
  other arithmetic  373 us (56%)
  local copies, waits for them, and re-layouts  181 us (27%)
  waiting for transfers between devices  109 us (16%)
  starting transfers between devices  8.18 us (1%)
    gather x1, local copies, waits for them, and re-layouts, per_device(): chosen = jnp.where(speed == local_best[cell], vehicle, VEHICLES)  181 us
    another operation x1, other arithmetic, per_device(): local_ident = jnp.full((CELLS,), VEHICLES, jnp.int32).at[cell].min(chosen)  176 us
    another operation x1, other arithmetic, per_device(): local_best = jnp.full((CELLS,), -1.0, jnp.float32).at[cell].max(speed)  172 us
    ppermute x5, waiting for transfers between devices, swapped(): return lax.ppermute(block, axis, route)  109 us
  transfers between devices with their start and end apart: 5, of which 5 were waited for; matrix products, arithmetic and copies ran while one was open for 0% of the time, Pallas kernels for 0%

commit v1 on v0

v1 whole, which is shorter than its diff:
```python
import jax
import jax.numpy as jnp
from jax import lax
from jax.sharding import PartitionSpec as P

CELLS = 524288
TOP = 65536
UNIT = 1024
EMPTY = (TOP + UNIT) * UNIT


def swapped(block, axis, apart):
    count = lax.axis_size(axis)
    route = []
    for low in range(count):
        high = low | 1 << apart
        if high != low and high < count:
            route += [(low, high), (high, low)]
    return lax.ppermute(block, axis, route)


def encode(speed, vehicle):
    return (TOP - (speed * UNIT).astype(jnp.int32)) * UNIT + vehicle


def decode(code):
    level = TOP - (code >> 10)
    return level.astype(jnp.float32) * (1.0 / UNIT), code & (UNIT - 1)


def finish(code):
    speed, vehicle = decode(code)
    return speed, jnp.where(speed < 0, -1, vehicle)


def dense(cell, code):
    buffer = jnp.full((CELLS,), EMPTY, jnp.int32).at[cell].min(code)
    outer = lax.axis_size("gx")
    inner = lax.axis_size("gy")
    nbits = (outer * inner).bit_length() - 1
    myself = lax.axis_index(("gx", "gy"))
    for level in reversed(range(nbits)):
        half = buffer.shape[0] // 2
        side = myself >> level & 1
        keep = lax.dynamic_slice_in_dim(buffer, side * half, half, 0)
        give = lax.dynamic_slice_in_dim(buffer, (1 - side) * half, half, 0)
        speed, vehicle = decode(give)
        partner = swapped(jnp.stack([speed, vehicle.astype(jnp.float32)]), ("gx", "gy"), level)
        buffer = jnp.minimum(keep, encode(partner[0], partner[1].astype(jnp.int32)))
    return finish(buffer)


def per_device(cell, vehicle, speed):
    return dense(cell, encode(speed, vehicle))


def solution(mesh):
    placed = (P(("gx", "gy")), P(("gx", "gy")), P(("gx", "gy")))
    return jax.shard_map(
        per_device,
        mesh=mesh,
        in_specs=placed,
        out_specs=(P(("gx", "gy")), P(("gx", "gy"))),
        check_vma=False,
    )
```

time: 672 us -> 309 us (0.46)
  other arithmetic: 373 us -> 190 us
  local copies, waits for them, and re-layouts: 181 us -> 0 us
    gather x1 -> x0, local copies, waits for them, and re-layouts: 181 us -> none  [per_device(): chosen = jnp.where(speed == local_best[cell], vehicle, VEHICLES)]
    another operation x7 -> x6, other arithmetic: 360 us -> 180 us  [the longest x1 175 us: dense(): buffer = jnp.full((CELLS,), EMPTY, jnp.int32).at[cell].min(code)]
    add x0 -> x5, other arithmetic: none -> 7.49 us  [encode(): return (TOP - (speed * UNIT).astype(jnp.int32)) * UNIT + vehicle]
where the time goes in v1:
time: 309 us
  other arithmetic  190 us (61%)
  waiting for transfers between devices  109 us (35%)
  starting transfers between devices  8.18 us (3%)
    another operation x1, other arithmetic, dense(): buffer = jnp.full((CELLS,), EMPTY, jnp.int32).at[cell].min(code)  175 us
    ppermute x5, waiting for transfers between devices, swapped(): return lax.ppermute(block, axis, route)  109 us
    ppermute x5, starting transfers between devices, swapped(): return lax.ppermute(block, axis, route)  8.18 us
    add x5, other arithmetic, encode(): return (TOP - (speed * UNIT).astype(jnp.int32)) * UNIT + vehicle  7.49 us
  transfers between devices with their start and end apart: 5, of which 5 were waited for; matrix products, arithmetic and copies ran while one was open for 0% of the time, Pallas kernels for 0%

profile of v1, /device:TPU:0, one launch (start us, length us, event | category | flops | bytes accessed | tf_op | source)
XLA Modules:
  0.0 308.6 jit_solution(2665924994374224238)
XLA Ops:
  0.6 1.1 compare_select_fusion
  1.7 175.5 %scatter_custom_fusion = s32[524288]{0:T(1024)S(1)} fusion(s32[32768]{0:T(1024)S(1)} %get-tuple-element.4, s32[32768]{0:T(1024)S(1)} %get-tuple-element.5, s32[]{:T(128)} %constant.24.clone.1), kind=kCustom, calls=%fused_computation.12 | custom fusion | flops 32768 | bytes 2097156 | tf_op jit(solution)/shard_map/scatter-min | solution.py:37
  177.2 0.1 convert_multiply_fusion
  177.4 2.9 pad_maximum_fusion
  180.4 3.0 collective-permute-start
  183.3 45.9 %collective-permute-done = f32[2,262144]{1,0:T(2,128)} collective-permute-done((f32[2,262144]{1,0:T(2,128)}, f32[2,262144]{1,0:T(2,128)}, u32[]{:S(2)}, u32[]{:S(2)}) %collective-permute-start) | collective-permute-done | bytes 2097184 | tf_op jit(solution)/shard_map/ppermute | solution.py:19
  229.3 4.9 %fusion = s32[1,262144]{1,0:T(1,128)S(1)} fusion(f32[2,262144]{1,0:T(2,128)} %collective-permute-done), kind=kLoop, calls=%fused_computation.3 | loop fusion | flops 1572864 | bytes 3145728 | tf_op jit(solution)/shard_map/add | solution.py:23
  234.2 0.1 dynamic-slice_minimum_fusion
  234.5 0.9 pad_maximum_fusion.1
  235.4 2.9 collective-permute-start.1
  238.3 44.9 %collective-permute-done.1 = f32[2,131072]{1,0:T(2,128)S(1)} collective-permute-done((f32[2,131072]{1,0:T(2,128)S(1)}, f32[2,131072]{1,0:T(2,128)S(1)}, u32[]{:S(2)}, u32[]{:S(2)}) %collective-permute-start.1) | collective-permute-done | bytes 1048608 | tf_op jit(solution)/shard_map/ppermute | solution.py:19
  283.2 1.4 fusion.6
  284.7 0.5 pad_maximum_fusion.2
  285.2 0.7 collective-permute-start.2
  285.9 12.2 %collective-permute-done.2 = f32[2,65536]{1,0:T(2,128)S(1)} collective-permute-done((f32[2,65536]{1,0:T(2,128)S(1)}, f32[2,65536]{1,0:T(2,128)S(1)}, u32[]{:S(2)}, u32[]{:S(2)}) %collective-permute-start.2) | collective-permute-done | bytes 524320 | tf_op jit(solution)/shard_map/ppermute | solution.py:19
  298.1 0.7 fusion.10
  298.9 0.2 pad_maximum_fusion.3
  299.2 1.5 collective-permute-start.3
  300.7 5.1 %collective-permute-done.3 = f32[2,32768]{1,0:T(2,128)S(1)} collective-permute-done((f32[2,32768]{1,0:T(2,128)S(1)}, f32[2,32768]{1,0:T(2,128)S(1)}, u32[]{:S(2)}, u32[]{:S(2)}) %collective-permute-start.3) | collective-permute-done | bytes 262176 | tf_op jit(solution)/shard_map/ppermute | solution.py:19
  305.8 0.3 fusion.14
  306.2 0.1 pad_maximum_fusion.4
  306.4 1.3 collective-permute-done.4
  307.7 0.2 fusion.18
  307.9 0.7 and_select_fusion
  (13 shorter events, 0.6 us)
Async XLA Ops:
  180.4 48.9 %collective-permute-start = (f32[2,262144]{1,0:T(2,128)}, f32[2,262144]{1,0:T(2,128)}, u32[]{:S(2)}, u32[]{:S(2)}) collective-permute-start(f32[2,262144]{1,0:T(2,128)} %pad_maximum_fusion), channel_id=1, source_target_pairs={{0,16},{16,0},{1,17},{17,1},{2,18},{18,2},{3,19},{19,3},{4,20},{20... | collective-permute-start | bytes 6291464 | tf_op jit(solution)/shard_map/ppermute | solution.py:19
  235.4 47.8 %collective-permute-start.1 = (f32[2,131072]{1,0:T(2,128)S(1)}, f32[2,131072]{1,0:T(2,128)S(1)}, u32[]{:S(2)}, u32[]{:S(2)}) collective-permute-start(f32[2,131072]{1,0:T(2,128)S(1)} %pad_maximum_fusion.1), channel_id=1, source_target_pairs={{0,8},{8,0},{1,9},{9,1},{2,10},{10,2},{3,11},{11,3},{4,12},{12,4},... | collective-permute-start | bytes 3145736 | tf_op jit(solution)/shard_map/ppermute | solution.py:19
  285.2 12.9 %collective-permute-start.2 = (f32[2,65536]{1,0:T(2,128)S(1)}, f32[2,65536]{1,0:T(2,128)S(1)}, u32[]{:S(2)}, u32[]{:S(2)}) collective-permute-start(f32[2,65536]{1,0:T(2,128)S(1)} %pad_maximum_fusion.2), channel_id=1, source_target_pairs={{0,4},{4,0},{1,5},{5,1},{2,6},{6,2},{3,7},{7,3},{8,12},{12,8},{9,1... | collective-permute-start | bytes 1572872 | tf_op jit(solution)/shard_map/ppermute | solution.py:19
  299.2 6.6 %collective-permute-start.3 = (f32[2,32768]{1,0:T(2,128)S(1)}, f32[2,32768]{1,0:T(2,128)S(1)}, u32[]{:S(2)}, u32[]{:S(2)}) collective-permute-start(f32[2,32768]{1,0:T(2,128)S(1)} %pad_maximum_fusion.3), channel_id=1, source_target_pairs={{0,2},{2,0},{1,3},{3,1},{4,6},{6,4},{5,7},{7,5},{8,10},{10,8},{9,1... | collective-permute-start | bytes 786440 | tf_op jit(solution)/shard_map/ppermute | solution.py:19
  306.3 1.4 collective-permute-start.4

commit v2 on v1

--- a/solution.py
+++ b/solution.py
@@ -1,12 +1,21 @@
+import functools
+
 import jax
 import jax.numpy as jnp
 from jax import lax
+from jax.experimental import pallas as pl
+from jax.experimental.pallas import tpu as pltpu
 from jax.sharding import PartitionSpec as P
 
 CELLS = 524288
 TOP = 65536
 UNIT = 1024
 EMPTY = (TOP + UNIT) * UNIT
+NONE = 1 << 30
+FAIL = -2
+SUBS = 8
+LANES = 128
+WIDE = 4
 
 
 def swapped(block, axis, apart):
@@ -33,7 +42,8 @@
     return speed, jnp.where(speed < 0, -1, vehicle)
 
 
-def dense(cell, code):
+def dense(cell, vehicle, speed):
+    code = encode(speed, vehicle)
     buffer = jnp.full((CELLS,), EMPTY, jnp.int32).at[cell].min(code)
     outer = lax.axis_size("gx")
     inner = lax.axis_size("gy")
@@ -50,8 +60,333 @@
     return finish(buffer)
 
 
+def lane_of():
+    return lax.broadcasted_iota(jnp.int32, (SUBS, LANES), 1)
+
+
+def sub_of():
+    return lax.broadcasted_iota(jnp.int32, (SUBS, LANES), 0)
+
+
+def before(c, k, pc, pk):
+    return (c < pc) | ((c == pc) & (k < pk))
+
+
+def exchange(c, k, pc, pk, high):
+    keep = jnp.logical_xor(before(c, k, pc, pk), high)
+    return jnp.where(keep, c, pc), jnp.where(keep, k, pk)
+
+
+def pair(x, y):
+    swap = before(y[0], y[1], x[0], x[1])
+    low = jnp.where(swap, y[0], x[0]), jnp.where(swap, y[1], x[1])
+    high = jnp.where(swap, x[0], y[0]), jnp.where(swap, x[1], y[1])
+    return low, high
+
+
+def turned(bit, vbits):
+    place = lane_of() * SUBS + sub_of()
+    return -((place >> (bit - vbits)) & 1)
+
+
+def merge_vregs(cs, ks, flip):
+    v = cs.shape[0]
+    half = v // 2
+    for i in range(half):
+        a, b = pair((cs[i], ks[i]), (cs[i + half], ks[i + half]))
+        cs[i], ks[i] = a
+        cs[i + half], ks[i + half] = b
+    for base in (0, half):
+        x = [(cs[base + i], ks[base + i]) for i in range(half)]
+        stride = half // 2
+        while stride:
+            for i in range(half):
+                if not i & stride:
+                    x[i], x[i + stride] = pair(x[i], x[i + stride])
+            stride //= 2
+        for i in range(half):
+            cs[base + i] = x[i][0] ^ flip
+            ks[base + i] = x[i][1] ^ flip
+
+
+def sort(cs, ks):
+    v = cs.shape[0]
+    half = v // 2
+    vbits = v.bit_length() - 1
+    total = vbits + 10
+    flip = turned(vbits, vbits)
+    for base in (0, half):
+        x = [(cs[base + i] ^ flip, ks[base + i] ^ flip) for i in range(half)]
+        for phase in range(1, vbits):
+            stride = 1 << (phase - 1)
+            while stride:
+                for i in range(half):
+                    if not i & stride:
+                        a, b = pair(x[i], x[i + stride])
+                        if (base + i) >> phase & 1:
+                            a, b = b, a
+                        x[i], x[i + stride] = a, b
+                stride //= 2
+        for i in range(half):
+            cs[base + i], ks[base + i] = x[i]
+    merge_vregs(cs, ks, turned(vbits, vbits) ^ turned(vbits + 1, vbits))
+    lane = lane_of()
+    sub = sub_of()
+
+    def sub_stage(j):
+        step = 1 << j
+        high = (sub & step) != 0
+
+        def partner(x):
+            up = pltpu.roll(x, step, 0)
+            if step * 2 == SUBS:
+                return up
+            return jnp.where(high, up, pltpu.roll(x, SUBS - step, 0))
+
+        for i in range(v):
+            c, k = cs[i], ks[i]
+            cs[i], ks[i] = exchange(c, k, partner(c), partner(k), high)
+
+    def lane_stage(n, bits):
+        step = jnp.int32(1) << (bits - 1 - n)
+        high = (lane & step) != 0
+        source = lane ^ step
+
+        def partner(x):
+            return jnp.take_along_axis(x, source, axis=1, mode="promise_in_bounds")
+
+        for i in range(v):
+            c, k = cs[i], ks[i]
+            cs[i], ks[i] = exchange(c, k, partner(c), partner(k), high)
+        return bits
+
+    def phase_body(phase, carry):
+        bits = jnp.maximum(phase - vbits - 3, 0)
+        lax.fori_loop(0, bits, lane_stage, bits)
+        for j in (2, 1, 0):
+            pl.when(phase - vbits - 1 >= j)(functools.partial(sub_stage, j))
+        merge_vregs(cs, ks, turned(phase, vbits) ^ turned(phase + 1, vbits))
+        return carry
+
+    lax.fori_loop(vbits + 1, total + 1, phase_body, 0)
+
+
+def earlier(x, q):
+    y = pltpu.roll(x, q, 0)
+    return jnp.where(sub_of() < q, pltpu.roll(y, 1, 1), y)
+
+
+def later(x, q):
+    y = pltpu.roll(x, SUBS - q, 0)
+    return jnp.where(sub_of() >= SUBS - q, pltpu.roll(y, LANES - 1, 1), y)
+
+
+def compress(cs, ks, ds, cs2, ks2, ds2):
+    v = cs.shape[0]
+    vbits = v.bit_length() - 1
+    lane = lane_of()
+    sub = sub_of()
+    start = (lane == 0) & (sub == 0)
+    count = jnp.zeros((SUBS, LANES), jnp.int32)
+    last = jnp.where(start, -1, earlier(cs[v - 1], 1))
+    for i in range(v):
+        c = cs[i]
+        lost = (c == last) | (c >= NONE)
+        ds[i] = jnp.where(lost, -1, count)
+        count = count + lost.astype(jnp.int32)
+        last = c
+    scan = count
+    for q in (1, 2, 4):
+        scan = scan + jnp.where(sub >= q, pltpu.roll(scan, q, 0), 0)
+    column = jnp.broadcast_to(scan[SUBS - 1 : SUBS, :], (SUBS, LANES))
+    run = column
+    for q in (1, 2, 4, 8, 16, 32, 64):
+        run = run + jnp.where(lane >= q, pltpu.roll(run, q, 1), 0)
+    offset = run - column + scan - count
+    for i in range(v):
+        d = ds[i]
+        cs[i] = jnp.where(d < 0, NONE, cs[i])
+        ds[i] = jnp.where(d < 0, 0, d + offset)
+
+    def step(own, inc, bit):
+        c, k, d = own
+        pc, pk, pd = inc
+        comes = (pd & bit) != 0
+        goes = (d & bit) != 0
+        return (
+            jnp.where(comes, pc, jnp.where(goes, NONE, c)),
+            jnp.where(comes, pk, k),
+            jnp.where(comes, pd, jnp.where(goes, 0, d)),
+        )
+
+    now, then = (cs, ks, ds), (cs2, ks2, ds2)
+    for b in range(vbits):
+        for i in range(v):
+            j = i + (1 << b)
+            own = tuple(r[i] for r in now)
+            inc = tuple(r[j] if j < v else later(r[j - v], 1) for r in now)
+            for r, x in zip(then, step(own, inc, 1 << b)):
+                r[i] = x
+        now, then = then, now
+    for b in range(3):
+        for i in range(v):
+            own = tuple(r[i] for r in now)
+            inc = tuple(later(x, 1 << b) for x in own)
+            for r, x in zip(now, step(own, inc, 1 << (b + vbits))):
+                r[i] = x
+
+    def lane_step(b, carry):
+        shift = LANES - (jnp.int32(1) << b)
+        for i in range(v):
+            own = tuple(r[i] for r in now)
+            inc = tuple(pltpu.roll(x, shift, 1) for x in own)
+            for r, x in zip(now, step(own, inc, jnp.int32(1) << (b + vbits + 3))):
+                r[i] = x
+        return carry
+
+    lax.fori_loop(0, 7, lane_step, 0)
+    return now, then
+
+
+def expand(ks, ds, ks2, ds2):
+    v = ks.shape[0]
+    vbits = v.bit_length() - 1
+
+    def step(own, inc, bit):
+        k, d = own
+        pk, pd = inc
+        comes = (pd & bit) != 0
+        goes = (d & bit) != 0
+        return (
+            jnp.where(comes, pk, jnp.where(goes, EMPTY, k)),
+            jnp.where(comes, pd, jnp.where(goes, 0, d)),
+        )
+
+    now, then = (ks, ds), (ks2, ds2)
+
+    def lane_step(n, carry):
+        b = 6 - n
+        for i in range(v):
+            own = tuple(r[i] for r in now)
+            inc = tuple(pltpu.roll(x, jnp.int32(1) << b, 1) for x in own)
+            for r, x in zip(now, step(own, inc, jnp.int32(1) << (b + vbits + 3))):
+                r[i] = x
+        return carry
+
+    lax.fori_loop(0, 7, lane_step, 0)
+    for b in (2, 1, 0):
+        for i in range(v):
+            own = tuple(r[i] for r in now)
+            inc = tuple(earlier(x, 1 << b) for x in own)
+            for r, x in zip(now, step(own, inc, 1 << (b + vbits))):
+                r[i] = x
+    for b in reversed(range(vbits)):
+        for i in range(v):
+            j = i - (1 << b)
+            own = tuple(r[i] for r in now)
+            inc = tuple(r[j] if j >= 0 else earlier(r[j + v], 1) for r in now)
+            for r, x in zip(then, step(own, inc, 1 << b)):
+                r[i] = x
+        now, then = then, now
+    return now[0]
+
+
+def send_kernel(n, cell_ref, vehicle_ref, speed_ref, out_ref, cs, ks, ds, cs2, ks2, ds2, tc, tk):
+    v = cs.shape[0]
+    own = CELLS // n
+    for i in range(v):
+        cs[i] = cell_ref[i]
+        ks[i] = encode(speed_ref[i], vehicle_ref[i])
+    sort(cs, ks)
+    (c, k, _), _ = compress(cs, ks, ds, cs2, ks2, ds2)
+    first = c[0][0:1, :]
+    parts = SUBS // WIDE
+    rows = v // parts
+    for h in range(parts):
+        tc[h] = jnp.transpose(c[h * rows : (h + 1) * rows].reshape(rows * SUBS, LANES))
+        tk[h] = jnp.transpose(k[h * rows : (h + 1) * rows].reshape(rows * SUBS, LANES))
+    ahead = [jnp.sum((first < o * own).astype(jnp.int32)) for o in range(n + 1)]
+    starts = [jnp.clip(ahead[o] - 1, 0, LANES - WIDE) for o in range(n)]
+    fails = jnp.int32(0)
+    for o in range(n):
+        fails = fails | (ahead[o + 1] > starts[o] + WIDE).astype(jnp.int32)
+    for o in range(n):
+        for h in range(parts):
+            c = tc[h, pl.ds(starts[o], WIDE), :]
+            k = tk[h, pl.ds(starts[o], WIDE), :]
+            at = h * WIDE
+            out_ref[o, at : at + WIDE, :] = jnp.where(fails > 0, FAIL, c)
+            out_ref[o, SUBS + at : SUBS + at + WIDE, :] = TOP - (k >> 10)
+            out_ref[o, 2 * SUBS + at : 2 * SUBS + at + WIDE, :] = k & (UNIT - 1)
+
+
+def owner_kernel(n, got_ref, speed_ref, vehicle_ref, fail_ref, cs, ks, ds, cs2, ks2, ds2, tall):
+    v = cs.shape[0]
+    vbits = v.bit_length() - 1
+    own = CELLS // n
+    base = (lax.axis_index("gx") * lax.axis_size("gy") + lax.axis_index("gy")) * own
+    least = jnp.zeros((SUBS, LANES), jnp.int32)
+    for i in range(v):
+        c = got_ref[i, 0:SUBS, :]
+        least = jnp.minimum(least, c)
+        c = c - base
+        cs[i] = jnp.where((c >= 0) & (c < own), c, NONE)
+        ks[i] = (TOP - got_ref[i, SUBS : 2 * SUBS, :]) * UNIT + got_ref[i, 2 * SUBS : 3 * SUBS, :]
+    fail_ref[...] = least
+    sort(cs, ks)
+    (c, k, d), (_, k2, d2) = compress(cs, ks, ds, cs2, ks2, ds2)
+    place = (lane_of() * SUBS + sub_of()) * v
+    for i in range(v):
+        empty = c[i] >= NONE
+        d[i] = jnp.where(empty, 0, c[i] - (place + i))
+        k[i] = jnp.where(empty, EMPTY, k[i])
+    done = expand(k, d, k2, d2)
+    for i in range(v):
+        tall[pl.Slice(i, SUBS, v), :] = done[i]
+    columns = own // (v * SUBS)
+    parts = v * SUBS // LANES
+    wide = jnp.transpose(tall[...])
+    for h in range(parts):
+        speed, vehicle = finish(wide[0:columns, h * LANES : (h + 1) * LANES])
+        speed_ref[pl.Slice(h, columns, parts), :] = speed
+        vehicle_ref[pl.Slice(h, columns, parts), :] = vehicle
+
+
+def sparse(cell, vehicle, speed, n):
+    v = cell.shape[0] // (SUBS * LANES)
+    own = CELLS // n
+    shape = (v, SUBS, LANES)
+    slots = [pltpu.VMEM(shape, jnp.int32)] * 6
+    turn = pltpu.VMEM((SUBS // WIDE, LANES, v * WIDE), jnp.int32)
+    sent = pl.pallas_call(
+        functools.partial(send_kernel, n),
+        out_shape=jax.ShapeDtypeStruct((n, 3 * SUBS, LANES), jnp.int32),
+        scratch_shapes=slots + [turn, turn],
+    )(cell.reshape(shape), vehicle.reshape(shape), speed.reshape(shape))
+    got = lax.all_to_all(sent, ("gx", "gy"), 0, 0)
+    best, ident, least = pl.pallas_call(
+        functools.partial(owner_kernel, n),
+        out_shape=(
+            jax.ShapeDtypeStruct((own // LANES, LANES), jnp.float32),
+            jax.ShapeDtypeStruct((own // LANES, LANES), jnp.int32),
+            jax.ShapeDtypeStruct((SUBS, LANES), jnp.int32),
+        ),
+        scratch_shapes=slots + [pltpu.VMEM((v * SUBS, LANES), jnp.int32)],
+    )(got)
+    return best.reshape(own), ident.reshape(own), jnp.min(least) < 0
+
+
 def per_device(cell, vehicle, speed):
-    return dense(cell, encode(speed, vehicle))
+    n = lax.axis_size("gx") * lax.axis_size("gy")
+    v = cell.shape[0] // (SUBS * LANES)
+    if v != n or v * WIDE != LANES or cell.shape[0] % (SUBS * LANES) or CELLS % (n * v * SUBS):
+        return dense(cell, vehicle, speed)
+    best, ident, failed = sparse(cell, vehicle, speed, n)
+    return lax.cond(
+        failed,
+        lambda: dense(cell, vehicle, speed),
+        lambda: (best, ident),
+    )
 
 
 def solution(mesh):

time: 309 us -> 49.4 us (0.16)
  other arithmetic: 190 us -> 1.31 us
  waiting for transfers between devices: 109 us -> 13.1 us
  Pallas kernels: 0 us -> 25 us
    another operation x6 -> x0, other arithmetic: 180 us -> none  [the longest x1 175 us: dense(): buffer = jnp.full((CELLS,), EMPTY, jnp.int32).at[cell].min(code)]
    ppermute x5 -> x0, waiting for transfers between devices: 109 us -> none  [swapped(): return lax.ppermute(block, axis, route)]
    pallas_call x0 -> x2, Pallas kernels: none -> 25 us  [the longest x1 13.1 us: sparse(): pl.pallas_call(functools.partial(owner_kernel, n), out_shape=(jax.ShapeDt...]
    all_to_all x0 -> x1, waiting for transfers between devices: none -> 13.1 us  [sparse(): got = lax.all_to_all(sent, ('gx', 'gy'), 0, 0)]
    ppermute x5 -> x0, starting transfers between devices: 8.18 us -> none  [swapped(): return lax.ppermute(block, axis, route)]
    add x5 -> x0, other arithmetic: 7.49 us -> none  [encode(): return (TOP - (speed * UNIT).astype(jnp.int32)) * UNIT + vehicle]
    all_to_all x0 -> x1, starting transfers between devices: none -> 7.33 us  [sparse(): got = lax.all_to_all(sent, ('gx', 'gy'), 0, 0)]
  transfers between devices with their start and end apart: 5 -> 1, of which waited for: 5 -> 1; matrix products, arithmetic and copies ran while one was open for 0% -> 0% of each run, Pallas kernels for 0% -> 0%
where the time goes in v2:
time: 49.4 us; the launch traced here: 49.1 us
  Pallas kernels  25 us (51%)
  waiting for transfers between devices  13.1 us (27%)
  starting transfers between devices  7.33 us (15%)
  between operations  1.39 us (3%)
  other arithmetic  1.31 us (3%)
  local copies, waits for them, and re-layouts  0.74 us (1%)
    pallas_call x1, Pallas kernels, sparse(): pl.pallas_call(functools.partial(owner_kernel, n), out_shape=(jax.ShapeDt...  13.1 us
    all_to_all x1, waiting for transfers between devices, sparse(): got = lax.all_to_all(sent, ('gx', 'gy'), 0, 0)  13.1 us
    pallas_call x1, Pallas kernels, sparse(): pl.pallas_call(functools.partial(send_kernel, n), out_shape=jax.ShapeDtyp...  11.9 us
    all_to_all x1, starting transfers between devices, sparse(): got = lax.all_to_all(sent, ('gx', 'gy'), 0, 0)  7.33 us
    reduce_min x1, other arithmetic, sparse(): return (best.reshape(own), ident.reshape(own), jnp.min(least) < 0)  1.31 us
  transfers between devices with their start and end apart: 1, of which 1 were waited for; matrix products, arithmetic and copies ran while one was open for 0% of the time, Pallas kernels for 0%

profile of v2, /device:TPU:0, one launch (start us, length us, event | category | flops | bytes accessed | tf_op | source)
XLA Modules:
  0.0 49.1 jit_solution(16644553046926444677)
XLA Ops:
  0.6 11.9 %shard_map.54 = s32[32,24,128]{2,1,0:T(8,128)} custom-call(s32[32,8,128]{2,1,0:T(8,128)} %bitcast.30, s32[32,8,128]{2,1,0:T(8,128)} %bitcast.31, f32[32,8,128]{2,1,0:T(8,128)} %bitcast.32), custom_call_target="tpu_custom_call" | custom-call | tf_op jit(solution)/shard_map/pallas_call | solution.py:361
  12.5 7.3 %all-to-all-start = ((s32[32,24,128]{2,1,0:T(8,128)}), s32[32,24,128]{2,1,0:T(8,128)S(1)}, u32[]{:S(2)}, u32[]{:S(2)}) async-start(s32[32,24,128]{2,1,0:T(8,128)} %shard_map.54), calls=%async_computation | async-start | bytes 786432 | tf_op jit(solution)/shard_map/all_to_all | solution.py:366
  19.9 13.1 %all-to-all-done.got_ref = s32[32,24,128]{2,1,0:T(8,128)S(1)} async-done(((s32[32,24,128]{2,1,0:T(8,128)}), s32[32,24,128]{2,1,0:T(8,128)S(1)}, u32[]{:S(2)}, u32[]{:S(2)}) %all-to-all-start) | async-done | bytes 393248 | tf_op jit(solution)/shard_map/all_to_all | solution.py:366
  32.9 0.0 copy-start
  32.9 0.7 %copy-done = s32[32,24,128]{2,1,0:T(8,128)} copy-done((s32[32,24,128]{2,1,0:T(8,128)}, s32[32,24,128]{2,1,0:T(8,128)S(1)}, u32[]{:S(2)}) %copy-start) | copy-done | bytes 393240
  33.7 13.1 %shard_map.55 = (f32[128,128]{1,0:T(8,128)}, s32[128,128]{1,0:T(8,128)}, s32[8,128]{1,0:T(8,128)}) custom-call(s32[32,24,128]{2,1,0:T(8,128)} %copy-done), custom_call_target="tpu_custom_call" | custom-call | tf_op jit(solution)/shard_map/pallas_call | solution.py:367
  46.8 1.3 %reduce_min.9 = s32[]{:T(128)} reduce(s32[8,128]{1,0:T(8,128)} %get-tuple-element.24, s32[]{:T(128)} %constant.48.clone.1), dimensions={0,1}, to_apply=%region_0.0 | reduce | flops 1023 | bytes 4104 | tf_op jit(solution)/shard_map/reduce_min | solution.py:376
  48.7 0.2 conditional.1
Async XLA Ops:
  12.5 20.4 %all-to-all-start = ((s32[32,24,128]{2,1,0:T(8,128)}), s32[32,24,128]{2,1,0:T(8,128)S(1)}, u32[]{:S(2)}, u32[]{:S(2)}) async-start(s32[32,24,128]{2,1,0:T(8,128)} %shard_map.54), calls=%async_computation | async-start | bytes 786432 | tf_op jit(solution)/shard_map/all_to_all | solution.py:366
  32.9 0.7 %copy-start = (s32[32,24,128]{2,1,0:T(8,128)}, s32[32,24,128]{2,1,0:T(8,128)S(1)}, u32[]{:S(2)}) copy-start(s32[32,24,128]{2,1,0:T(8,128)S(1)} %all-to-all-done.got_ref) | copy-start | bytes 1179652

commit v3 on v2

--- a/solution.py
+++ b/solution.py
@@ -12,7 +12,7 @@
 UNIT = 1024
 EMPTY = (TOP + UNIT) * UNIT
 NONE = 1 << 30
-FAIL = -2
+FAIL = -2000000000
 SUBS = 8
 LANES = 128
 WIDE = 4
@@ -130,6 +130,13 @@
         for i in range(half):
             cs[base + i], ks[base + i] = x[i]
     merge_vregs(cs, ks, turned(vbits, vbits) ^ turned(vbits + 1, vbits))
+    merge_phases(cs, ks, vbits + 1)
+
+
+def merge_phases(cs, ks, begin):
+    v = cs.shape[0]
+    vbits = v.bit_length() - 1
+    total = vbits + 10
     lane = lane_of()
     sub = sub_of()
 
@@ -164,11 +171,14 @@
         bits = jnp.maximum(phase - vbits - 3, 0)
         lax.fori_loop(0, bits, lane_stage, bits)
         for j in (2, 1, 0):
-            pl.when(phase - vbits - 1 >= j)(functools.partial(sub_stage, j))
+            if begin - vbits - 1 >= j:
+                sub_stage(j)
+            else:
+                pl.when(phase - vbits - 1 >= j)(functools.partial(sub_stage, j))
         merge_vregs(cs, ks, turned(phase, vbits) ^ turned(phase + 1, vbits))
         return carry
 
-    lax.fori_loop(vbits + 1, total + 1, phase_body, 0)
+    lax.fori_loop(begin, total + 1, phase_body, 0)
 
 
 def earlier(x, q):
@@ -181,17 +191,17 @@
     return jnp.where(sub_of() >= SUBS - q, pltpu.roll(y, LANES - 1, 1), y)
 
 
-def compress(cs, ks, ds, cs2, ks2, ds2):
+def compress(limit, cs, ks, ds, cs2, ks2, ds2):
     v = cs.shape[0]
     vbits = v.bit_length() - 1
     lane = lane_of()
     sub = sub_of()
     start = (lane == 0) & (sub == 0)
     count = jnp.zeros((SUBS, LANES), jnp.int32)
-    last = jnp.where(start, -1, earlier(cs[v - 1], 1))
+    last = jnp.where(start, FAIL, earlier(cs[v - 1], 1))
     for i in range(v):
         c = cs[i]
-        lost = (c == last) | (c >= NONE)
+        lost = (c == last) | (c < 0) | (c >= limit)
         ds[i] = jnp.where(lost, -1, count)
         count = count + lost.astype(jnp.int32)
         last = c
@@ -291,14 +301,20 @@
     return now[0]
 
 
+def myself():
+    return lax.axis_index("gx") * lax.axis_size("gy") + lax.axis_index("gy")
+
+
 def send_kernel(n, cell_ref, vehicle_ref, speed_ref, out_ref, cs, ks, ds, cs2, ks2, ds2, tc, tk):
     v = cs.shape[0]
     own = CELLS // n
+    odd = myself() & 1
     for i in range(v):
-        cs[i] = cell_ref[i]
+        c = cell_ref[i]
+        cs[i] = jnp.where(odd == 1, CELLS - 1 - c, c)
         ks[i] = encode(speed_ref[i], vehicle_ref[i])
     sort(cs, ks)
-    (c, k, _), _ = compress(cs, ks, ds, cs2, ks2, ds2)
+    (c, k, _), _ = compress(CELLS, cs, ks, ds, cs2, ks2, ds2)
     first = c[0][0:1, :]
     parts = SUBS // WIDE
     rows = v // parts
@@ -310,31 +326,73 @@
     fails = jnp.int32(0)
     for o in range(n):
         fails = fails | (ahead[o + 1] > starts[o] + WIDE).astype(jnp.int32)
-    for o in range(n):
+    for q in range(n):
+        o = jnp.where(odd == 1, n - 1 - q, q)
         for h in range(parts):
-            c = tc[h, pl.ds(starts[o], WIDE), :]
-            k = tk[h, pl.ds(starts[o], WIDE), :]
+            c = tc[h, pl.ds(starts[q], WIDE), :]
+            k = jnp.where(c >= NONE, 0, tk[h, pl.ds(starts[q], WIDE), :])
+            c = jnp.where(odd == 1, CELLS - 1 - c, c)
             at = h * WIDE
             out_ref[o, at : at + WIDE, :] = jnp.where(fails > 0, FAIL, c)
             out_ref[o, SUBS + at : SUBS + at + WIDE, :] = TOP - (k >> 10)
             out_ref[o, 2 * SUBS + at : 2 * SUBS + at + WIDE, :] = k & (UNIT - 1)
 
 
+def swap_kernel(n, sent, got, send_sem, recv_sem):
+    me = myself()
+    inner = lax.axis_size("gy")
+
+    def spot(device):
+        return (device // inner, device % inner)
+
+    barrier = pltpu.get_barrier_semaphore()
+    for k in range(1, n):
+        pl.semaphore_signal(barrier, inc=1, device_id=spot(me ^ k), device_id_type=pl.DeviceIdType.MESH)
+    mine = pltpu.make_async_copy(sent.at[me], got.at[me], send_sem.at[0])
+    mine.start()
+    pl.semaphore_wait(barrier, n - 1)
+    copies = []
+    for k in range(1, n):
+        copy = pltpu.make_async_remote_copy(
+            src_ref=sent.at[me ^ k],
+            dst_ref=got.at[me],
+            send_sem=send_sem.at[k],
+            recv_sem=recv_sem.at[k],
+            device_id=spot(me ^ k),
+            device_id_type=pl.DeviceIdType.MESH,
+        )
+        copy.start()
+        copies.append(copy)
+    mine.wait()
+    for copy in copies:
+        copy.wait()
+
+
 def owner_kernel(n, got_ref, speed_ref, vehicle_ref, fail_ref, cs, ks, ds, cs2, ks2, ds2, tall):
     v = cs.shape[0]
     vbits = v.bit_length() - 1
     own = CELLS // n
-    base = (lax.axis_index("gx") * lax.axis_size("gy") + lax.axis_index("gy")) * own
+    base = myself() * own
+    parts = SUBS // WIDE
+    rows = v // parts
+    begin = vbits + 3 + WIDE.bit_length()
+    flip = turned(begin, vbits)
     least = jnp.zeros((SUBS, LANES), jnp.int32)
-    for i in range(v):
-        c = got_ref[i, 0:SUBS, :]
-        least = jnp.minimum(least, c)
-        c = c - base
-        cs[i] = jnp.where((c >= 0) & (c < own), c, NONE)
-        ks[i] = (TOP - got_ref[i, SUBS : 2 * SUBS, :]) * UNIT + got_ref[i, 2 * SUBS : 3 * SUBS, :]
-    fail_ref[...] = least
-    sort(cs, ks)
-    (c, k, d), (_, k2, d2) = compress(cs, ks, ds, cs2, ks2, ds2)
+    for h in range(parts):
+        at = h * WIDE
+        c = got_ref[:, at : at + WIDE, :].reshape(v * WIDE, LANES)
+        level = got_ref[:, SUBS + at : SUBS + at + WIDE, :].reshape(v * WIDE, LANES)
+        vehicle = got_ref[:, 2 * SUBS + at : 2 * SUBS + at + WIDE, :].reshape(v * WIDE, LANES)
+        k = (TOP - level) * UNIT + vehicle
+        least = jnp.minimum(least, jnp.min(c.reshape(v * WIDE // SUBS, SUBS, LANES), axis=0))
+        c = jnp.transpose(c - base).reshape(rows, SUBS, LANES)
+        k = jnp.transpose(k).reshape(rows, SUBS, LANES)
+        for i in range(rows):
+            cs[h * rows + i] = c[i] ^ flip
+            ks[h * rows + i] = k[i] ^ flip
+    fail_ref[0] = (jnp.min(least) == FAIL).astype(jnp.int32)
+    merge_phases(cs, ks, begin)
+    (c, k, d), (_, k2, d2) = compress(own, cs, ks, ds, cs2, ks2, ds2)
     place = (lane_of() * SUBS + sub_of()) * v
     for i in range(v):
         empty = c[i] >= NONE
@@ -363,17 +421,32 @@
         out_shape=jax.ShapeDtypeStruct((n, 3 * SUBS, LANES), jnp.int32),
         scratch_shapes=slots + [turn, turn],
     )(cell.reshape(shape), vehicle.reshape(shape), speed.reshape(shape))
-    got = lax.all_to_all(sent, ("gx", "gy"), 0, 0)
-    best, ident, least = pl.pallas_call(
+    got = pl.pallas_call(
+        functools.partial(swap_kernel, n),
+        out_shape=jax.ShapeDtypeStruct(sent.shape, sent.dtype),
+        in_specs=[pl.BlockSpec(memory_space=pltpu.VMEM)],
+        out_specs=pl.BlockSpec(memory_space=pltpu.VMEM),
+        scratch_shapes=[
+            pltpu.SemaphoreType.DMA((n,)),
+            pltpu.SemaphoreType.DMA((n,)),
+        ],
+        compiler_params=pltpu.CompilerParams(collective_id=0, has_side_effects=True),
+    )(sent)
+    best, ident, fail = pl.pallas_call(
         functools.partial(owner_kernel, n),
         out_shape=(
             jax.ShapeDtypeStruct((own // LANES, LANES), jnp.float32),
             jax.ShapeDtypeStruct((own // LANES, LANES), jnp.int32),
-            jax.ShapeDtypeStruct((SUBS, LANES), jnp.int32),
+            jax.ShapeDtypeStruct((1,), jnp.int32),
+        ),
+        out_specs=(
+            pl.BlockSpec(memory_space=pltpu.VMEM),
+            pl.BlockSpec(memory_space=pltpu.VMEM),
+            pl.BlockSpec(memory_space=pltpu.SMEM),
         ),
         scratch_shapes=slots + [pltpu.VMEM((v * SUBS, LANES), jnp.int32)],
     )(got)
-    return best.reshape(own), ident.reshape(own), jnp.min(least) < 0
+    return best.reshape(own), ident.reshape(own), fail[0] > 0
 
 
 def per_device(cell, vehicle, speed):

time: 49.4 us -> 43.5 us (0.88)
  Pallas kernels: 25 us -> 41.6 us
  waiting for transfers between devices: 13.1 us -> 0 us
  starting transfers between devices: 7.33 us -> 0 us
  other arithmetic: 1.31 us -> 0 us
  local copies, waits for them, and re-layouts: 0.74 us -> 0 us
    pallas_call x0 -> x1, Pallas kernels: none -> 18.5 us  [sparse(): pl.pallas_call(functools.partial(swap_kernel, n), out_shape=jax.ShapeDtyp...]
    all_to_all x1 -> x0, waiting for transfers between devices: 13.1 us -> none  [sparse(): got = lax.all_to_all(sent, ('gx', 'gy'), 0, 0)]
    all_to_all x1 -> x0, starting transfers between devices: 7.33 us -> none  [sparse(): got = lax.all_to_all(sent, ('gx', 'gy'), 0, 0)]
    pallas_call x1, Pallas kernels: 13.1 us -> 11.1 us  [sparse(): pl.pallas_call(functools.partial(owner_kernel, n), out_shape=(jax.ShapeDt...]
    reduce_min x1 -> x0, other arithmetic: 1.31 us -> none  [sparse(): return (best.reshape(own), ident.reshape(own), jnp.min(least) < 0)]
    unnamed x2 -> x0, local copies, waits for them, and re-layouts: 0.74 us -> none
  transfers between devices with their start and end apart: 1 -> 0, of which waited for: 1 -> 0; matrix products, arithmetic and copies ran while one was open for 0% -> 0% of each run, Pallas kernels for 0% -> 0%
where the time goes in v3:
time: 43.5 us; the launch traced here: 43.3 us
  Pallas kernels  41.6 us (96%)
  between operations  1.52 us (3%)
    pallas_call x1, Pallas kernels, sparse(): pl.pallas_call(functools.partial(swap_kernel, n), out_shape=jax.ShapeDtyp...  18.5 us
    pallas_call x1, Pallas kernels, sparse(): pl.pallas_call(functools.partial(send_kernel, n), out_shape=jax.ShapeDtyp...  11.9 us
    pallas_call x1, Pallas kernels, sparse(): pl.pallas_call(functools.partial(owner_kernel, n), out_shape=(jax.ShapeDt...  11.1 us

profile of v3, /device:TPU:0, one launch (start us, length us, event | category | flops | bytes accessed | tf_op | source)
XLA Modules:
  0.0 43.3 jit_solution(13569698875044268542)
XLA Ops:
  0.6 11.9 %shard_map.54.sent = s32[32,24,128]{2,1,0:T(8,128)} custom-call(s32[32,8,128]{2,1,0:T(8,128)} %bitcast.31, s32[32,8,128]{2,1,0:T(8,128)} %bitcast.32, f32[32,8,128]{2,1,0:T(8,128)} %bitcast.33), custom_call_target="tpu_custom_call" | custom-call | tf_op jit(solution)/shard_map/pallas_call | solution.py:419
  12.6 18.5 %shard_map.55.got_ref = s32[32,24,128]{2,1,0:T(8,128)} custom-call(s32[32,24,128]{2,1,0:T(8,128)} %shard_map.54.sent), custom_call_target="tpu_custom_call" | custom-call | tf_op jit(solution)/shard_map/pallas_call | solution.py:424
  31.1 11.1 %shard_map.56 = (f32[128,128]{1,0:T(8,128)}, s32[128,128]{1,0:T(8,128)}, s32[1]{0:T(128)}) custom-call(s32[32,24,128]{2,1,0:T(8,128)} %shard_map.55.got_ref), custom_call_target="tpu_custom_call" | custom-call | tf_op jit(solution)/shard_map/pallas_call | solution.py:435
  42.9 0.2 conditional.1

commit v4 on v3

--- a/solution.py
+++ b/solution.py
@@ -16,6 +16,8 @@
 SUBS = 8
 LANES = 128
 WIDE = 4
+ROWS = 5
+ORDER = (0, 2, 4, 1, 3)
 
 
 def swapped(block, axis, apart):
@@ -305,7 +307,16 @@
     return lax.axis_index("gx") * lax.axis_size("gy") + lax.axis_index("gy")
 
 
-def send_kernel(n, cell_ref, vehicle_ref, speed_ref, out_ref, cs, ks, ds, cs2, ks2, ds2, tc, tk):
+def flat(x, tall, out):
+    v = x.shape[0]
+    parts = v * SUBS // LANES
+    for i in range(v):
+        tall[pl.Slice(i, SUBS, v), :] = x[i]
+    for h in range(parts):
+        out[pl.Slice(h, LANES, parts), :] = jnp.transpose(tall[h * LANES : (h + 1) * LANES, :])
+
+
+def send_kernel(n, cell_ref, vehicle_ref, speed_ref, out_ref, cs, ks, ds, cs2, ks2, ds2, tall, tc, tk):
     v = cs.shape[0]
     own = CELLS // n
     odd = myself() & 1
@@ -315,27 +326,41 @@
         ks[i] = encode(speed_ref[i], vehicle_ref[i])
     sort(cs, ks)
     (c, k, _), _ = compress(CELLS, cs, ks, ds, cs2, ks2, ds2)
-    first = c[0][0:1, :]
-    parts = SUBS // WIDE
-    rows = v // parts
-    for h in range(parts):
-        tc[h] = jnp.transpose(c[h * rows : (h + 1) * rows].reshape(rows * SUBS, LANES))
-        tk[h] = jnp.transpose(k[h * rows : (h + 1) * rows].reshape(rows * SUBS, LANES))
-    ahead = [jnp.sum((first < o * own).astype(jnp.int32)) for o in range(n + 1)]
-    starts = [jnp.clip(ahead[o] - 1, 0, LANES - WIDE) for o in range(n)]
+    flat(c, tall, tc)
+    flat(k, tall, tk)
+    heads = LANES // v
+    lead = [c[0][s : s + 1, :] for s in range(0, SUBS, heads)]
+    tc[v * SUBS : (v + 1) * SUBS, :] = jnp.full((SUBS, LANES), NONE, jnp.int32)
+    starts = []
+    offs = []
+    for q in range(n + 1):
+        ahead = sum((x < q * own).astype(jnp.int32) for x in lead)
+        starts.append(jnp.maximum(jnp.sum(ahead) - 1, 0))
+    for q in range(n + 1):
+        row = tc[pl.ds(starts[q], 1), :]
+        offs.append(jnp.sum((row < q * own).astype(jnp.int32)))
     fails = jnp.int32(0)
-    for o in range(n):
-        fails = fails | (ahead[o + 1] > starts[o] + WIDE).astype(jnp.int32)
+    for q in range(n):
+        size = (starts[q + 1] - starts[q]) * LANES + offs[q + 1] - offs[q]
+        fails = fails | (size > ROWS * LANES).astype(jnp.int32)
+    lane = lane_of()
     for q in range(n):
         o = jnp.where(odd == 1, n - 1 - q, q)
-        for h in range(parts):
-            c = tc[h, pl.ds(starts[q], WIDE), :]
-            k = jnp.where(c >= NONE, 0, tk[h, pl.ds(starts[q], WIDE), :])
-            c = jnp.where(odd == 1, CELLS - 1 - c, c)
-            at = h * WIDE
-            out_ref[o, at : at + WIDE, :] = jnp.where(fails > 0, FAIL, c)
-            out_ref[o, SUBS + at : SUBS + at + WIDE, :] = TOP - (k >> 10)
-            out_ref[o, 2 * SUBS + at : 2 * SUBS + at + WIDE, :] = k & (UNIT - 1)
+        tail = lane >= LANES - offs[q]
+
+        def window(ref):
+            x = pltpu.roll(ref[pl.ds(starts[q], SUBS), :], (LANES - offs[q]) & (LANES - 1), 1)
+            return jnp.where(tail, pltpu.roll(x, SUBS - 1, 0), x)
+
+        c = window(tc)
+        k = jnp.where(c >= NONE, 0, window(tk))
+        c = jnp.where(odd == 1, CELLS - 1 - c, c)
+        c = jnp.where(fails > 0, FAIL, c)
+        for at, w in enumerate(ORDER):
+            out_ref[o, at : at + 1, :] = c[w : w + 1, :]
+            out_ref[o, ROWS + at : ROWS + at + 1, :] = TOP - (k[w : w + 1, :] >> 10)
+            out_ref[o, 2 * ROWS + at : 2 * ROWS + at + 1, :] = k[w : w + 1, :] & (UNIT - 1)
+        out_ref[o, 3 * ROWS : 3 * ROWS + 1, :] = c[0:1, :]
 
 
 def swap_kernel(n, sent, got, send_sem, recv_sem):
@@ -368,28 +393,35 @@
         copy.wait()
 
 
-def owner_kernel(n, got_ref, speed_ref, vehicle_ref, fail_ref, cs, ks, ds, cs2, ks2, ds2, tall):
+def owner_kernel(n, got_ref, speed_ref, vehicle_ref, fail_ref, cs, ks, ds, cs2, ks2, ds2, tall, uc, uk):
     v = cs.shape[0]
     vbits = v.bit_length() - 1
     own = CELLS // n
     base = myself() * own
-    parts = SUBS // WIDE
-    rows = v // parts
     begin = vbits + 3 + WIDE.bit_length()
     flip = turned(begin, vbits)
-    least = jnp.zeros((SUBS, LANES), jnp.int32)
+    parts = v * SUBS // LANES
+    least = jnp.zeros((1, LANES), jnp.int32)
+    edge = lax.broadcasted_iota(jnp.int32, (v * WIDE, LANES), 0)
+    pad = jnp.where((edge // WIDE) % 2 == 1, -NONE, NONE)
     for h in range(parts):
-        at = h * WIDE
-        c = got_ref[:, at : at + WIDE, :].reshape(v * WIDE, LANES)
-        level = got_ref[:, SUBS + at : SUBS + at + WIDE, :].reshape(v * WIDE, LANES)
-        vehicle = got_ref[:, 2 * SUBS + at : 2 * SUBS + at + WIDE, :].reshape(v * WIDE, LANES)
-        k = (TOP - level) * UNIT + vehicle
-        least = jnp.minimum(least, jnp.min(c.reshape(v * WIDE // SUBS, SUBS, LANES), axis=0))
-        c = jnp.transpose(c - base).reshape(rows, SUBS, LANES)
-        k = jnp.transpose(k).reshape(rows, SUBS, LANES)
-        for i in range(rows):
-            cs[h * rows + i] = c[i] ^ flip
-            ks[h * rows + i] = k[i] ^ flip
+        uc[h] = pad
+        uk[h] = jnp.zeros_like(pad)
+    first = ROWS - ROWS // 2
+    for o in range(n):
+        c = got_ref[o, 0:ROWS, :]
+        k = (TOP - got_ref[o, ROWS : 2 * ROWS, :]) * UNIT + got_ref[o, 2 * ROWS : 3 * ROWS, :]
+        least = jnp.minimum(least, c[0:1, :])
+        c = c - base
+        uc[0, o * WIDE : o * WIDE + first, :] = c[0:first]
+        uk[0, o * WIDE : o * WIDE + first, :] = k[0:first]
+        uc[1, o * WIDE : o * WIDE + ROWS - first, :] = c[first:ROWS]
+        uk[1, o * WIDE : o * WIDE + ROWS - first, :] = k[first:ROWS]
+    for ref, out in ((uc, cs), (uk, ks)):
+        for h in range(parts):
+            tall[h * LANES : (h + 1) * LANES, :] = jnp.transpose(ref[h])
+        for i in range(v):
+            out[i] = tall[pl.Slice(i, SUBS, v), :] ^ flip
     fail_ref[0] = (jnp.min(least) == FAIL).astype(jnp.int32)
     merge_phases(cs, ks, begin)
     (c, k, d), (_, k2, d2) = compress(own, cs, ks, ds, cs2, ks2, ds2)
@@ -415,11 +447,13 @@
     own = CELLS // n
     shape = (v, SUBS, LANES)
     slots = [pltpu.VMEM(shape, jnp.int32)] * 6
-    turn = pltpu.VMEM((SUBS // WIDE, LANES, v * WIDE), jnp.int32)
+    tall = pltpu.VMEM((v * SUBS, LANES), jnp.int32)
+    rows = pltpu.VMEM(((v + 1) * SUBS, LANES), jnp.int32)
+    runs = pltpu.VMEM((v * SUBS // LANES, v * WIDE, LANES), jnp.int32)
     sent = pl.pallas_call(
         functools.partial(send_kernel, n),
-        out_shape=jax.ShapeDtypeStruct((n, 3 * SUBS, LANES), jnp.int32),
-        scratch_shapes=slots + [turn, turn],
+        out_shape=jax.ShapeDtypeStruct((n, 2 * SUBS, LANES), jnp.int32),
+        scratch_shapes=slots + [tall, rows, rows],
     )(cell.reshape(shape), vehicle.reshape(shape), speed.reshape(shape))
     got = pl.pallas_call(
         functools.partial(swap_kernel, n),
@@ -444,7 +478,7 @@
             pl.BlockSpec(memory_space=pltpu.VMEM),
             pl.BlockSpec(memory_space=pltpu.SMEM),
         ),
-        scratch_shapes=slots + [pltpu.VMEM((v * SUBS, LANES), jnp.int32)],
+        scratch_shapes=slots + [tall, runs, runs],
     )(got)
     return best.reshape(own), ident.reshape(own), fail[0] > 0
 

time: 43.5 us -> 41.2 us (0.947)
  Pallas kernels: 41.6 us -> 39.3 us
    pallas_call x1, Pallas kernels: 18.5 us -> 15.9 us  [sparse(): pl.pallas_call(functools.partial(swap_kernel, n), out_shape=jax.ShapeDtyp...]
where the time goes in v4:
time: 41.2 us; the launch traced here: 41 us
  Pallas kernels  39.3 us (95%)
  between operations  1.45 us (4%)
    pallas_call x1, Pallas kernels, sparse(): pl.pallas_call(functools.partial(swap_kernel, n), out_shape=jax.ShapeDtyp...  15.9 us
    pallas_call x1, Pallas kernels, sparse(): pl.pallas_call(functools.partial(send_kernel, n), out_shape=jax.ShapeDtyp...  12.2 us
    pallas_call x1, Pallas kernels, sparse(): pl.pallas_call(functools.partial(owner_kernel, n), out_shape=(jax.ShapeDt...  11.2 us

profile of v4, /device:TPU:0, one launch (start us, length us, event | category | flops | bytes accessed | tf_op | source)
XLA Modules:
  0.0 41.0 jit_solution(11878852350280793990)
XLA Ops:
  0.6 12.2 %shard_map.54.sent = s32[32,16,128]{2,1,0:T(8,128)} custom-call(s32[32,8,128]{2,1,0:T(8,128)} %bitcast.30, s32[32,8,128]{2,1,0:T(8,128)} %bitcast.31, f32[32,8,128]{2,1,0:T(8,128)} %bitcast.32), custom_call_target="tpu_custom_call" | custom-call | tf_op jit(solution)/shard_map/pallas_call | solution.py:453
  12.9 15.9 %shard_map.55.got_ref = s32[32,16,128]{2,1,0:T(8,128)} custom-call(s32[32,16,128]{2,1,0:T(8,128)} %shard_map.54.sent), custom_call_target="tpu_custom_call" | custom-call | tf_op jit(solution)/shard_map/pallas_call | solution.py:458
  28.8 11.2 %shard_map.56 = (f32[128,128]{1,0:T(8,128)}, s32[128,128]{1,0:T(8,128)}, s32[1]{0:T(128)}) custom-call(s32[32,16,128]{2,1,0:T(8,128)} %shard_map.55.got_ref), custom_call_target="tpu_custom_call" | custom-call | tf_op jit(solution)/shard_map/pallas_call | solution.py:469
  40.6 0.2 conditional.1

commit v5 on v4

--- a/solution.py
+++ b/solution.py
@@ -15,6 +15,7 @@
 FAIL = -2000000000
 SUBS = 8
 LANES = 128
+GRANT = 16 << 20
 WIDE = 4
 ROWS = 5
 ORDER = (0, 2, 4, 1, 3)
@@ -156,8 +157,8 @@
             c, k = cs[i], ks[i]
             cs[i], ks[i] = exchange(c, k, partner(c), partner(k), high)
 
-    def lane_stage(n, bits):
-        step = jnp.int32(1) << (bits - 1 - n)
+    def lane_stage(bit):
+        step = 1 << bit
         high = (lane & step) != 0
         source = lane ^ step
 
@@ -167,20 +168,14 @@
         for i in range(v):
             c, k = cs[i], ks[i]
             cs[i], ks[i] = exchange(c, k, partner(c), partner(k), high)
-        return bits
-
-    def phase_body(phase, carry):
-        bits = jnp.maximum(phase - vbits - 3, 0)
-        lax.fori_loop(0, bits, lane_stage, bits)
+
+    for phase in range(begin, total + 1):
+        for bit in reversed(range(phase - vbits - 3)):
+            lane_stage(bit)
         for j in (2, 1, 0):
-            if begin - vbits - 1 >= j:
+            if phase - vbits - 1 >= j:
                 sub_stage(j)
-            else:
-                pl.when(phase - vbits - 1 >= j)(functools.partial(sub_stage, j))
         merge_vregs(cs, ks, turned(phase, vbits) ^ turned(phase + 1, vbits))
-        return carry
-
-    lax.fori_loop(begin, total + 1, phase_body, 0)
 
 
 def earlier(x, q):
@@ -247,16 +242,13 @@
             for r, x in zip(now, step(own, inc, 1 << (b + vbits))):
                 r[i] = x
 
-    def lane_step(b, carry):
-        shift = LANES - (jnp.int32(1) << b)
+    for b in range(7):
+        shift = LANES - (1 << b)
         for i in range(v):
             own = tuple(r[i] for r in now)
             inc = tuple(pltpu.roll(x, shift, 1) for x in own)
-            for r, x in zip(now, step(own, inc, jnp.int32(1) << (b + vbits + 3))):
-                r[i] = x
-        return carry
-
-    lax.fori_loop(0, 7, lane_step, 0)
+            for r, x in zip(now, step(own, inc, 1 << (b + vbits + 3))):
+                r[i] = x
     return now, then
 
 
@@ -276,16 +268,12 @@
 
     now, then = (ks, ds), (ks2, ds2)
 
-    def lane_step(n, carry):
-        b = 6 - n
-        for i in range(v):
-            own = tuple(r[i] for r in now)
-            inc = tuple(pltpu.roll(x, jnp.int32(1) << b, 1) for x in own)
-            for r, x in zip(now, step(own, inc, jnp.int32(1) << (b + vbits + 3))):
-                r[i] = x
-        return carry
-
-    lax.fori_loop(0, 7, lane_step, 0)
+    for b in reversed(range(7)):
+        for i in range(v):
+            own = tuple(r[i] for r in now)
+            inc = tuple(pltpu.roll(x, 1 << b, 1) for x in own)
+            for r, x in zip(now, step(own, inc, 1 << (b + vbits + 3))):
+                r[i] = x
     for b in (2, 1, 0):
         for i in range(v):
             own = tuple(r[i] for r in now)
@@ -377,7 +365,7 @@
     mine.start()
     pl.semaphore_wait(barrier, n - 1)
     copies = []
-    for k in range(1, n):
+    for k in sorted(range(1, n), key=lambda k: -(k % inner)):
         copy = pltpu.make_async_remote_copy(
             src_ref=sent.at[me ^ k],
             dst_ref=got.at[me],
@@ -453,6 +441,7 @@
     sent = pl.pallas_call(
         functools.partial(send_kernel, n),
         out_shape=jax.ShapeDtypeStruct((n, 2 * SUBS, LANES), jnp.int32),
+        compiler_params=pltpu.CompilerParams(vmem_limit_bytes=GRANT),
         scratch_shapes=slots + [tall, rows, rows],
     )(cell.reshape(shape), vehicle.reshape(shape), speed.reshape(shape))
     got = pl.pallas_call(
@@ -464,7 +453,7 @@
             pltpu.SemaphoreType.DMA((n,)),
             pltpu.SemaphoreType.DMA((n,)),
         ],
-        compiler_params=pltpu.CompilerParams(collective_id=0, has_side_effects=True),
+        compiler_params=pltpu.CompilerParams(collective_id=0, has_side_effects=True, vmem_limit_bytes=GRANT),
     )(sent)
     best, ident, fail = pl.pallas_call(
         functools.partial(owner_kernel, n),
@@ -478,6 +467,7 @@
             pl.BlockSpec(memory_space=pltpu.VMEM),
             pl.BlockSpec(memory_space=pltpu.SMEM),
         ),
+        compiler_params=pltpu.CompilerParams(vmem_limit_bytes=GRANT),
         scratch_shapes=slots + [tall, runs, runs],
     )(got)
     return best.reshape(own), ident.reshape(own), fail[0] > 0

time: 41.2 us -> 32.7 us (0.79)
  Pallas kernels: 39.3 us -> 31.2 us
    pallas_call x1, Pallas kernels: 11.2 us -> 7.39 us  [sparse(): pl.pallas_call(functools.partial(owner_kernel, n), out_shape=(jax.ShapeDt...]
    pallas_call x1, Pallas kernels: 12.2 us -> 8.8 us  [sparse(): pl.pallas_call(functools.partial(send_kernel, n), out_shape=jax.ShapeDtyp...]
    pallas_call x1, Pallas kernels: 15.9 us -> 15 us  [sparse(): pl.pallas_call(functools.partial(swap_kernel, n), out_shape=jax.ShapeDtyp...]
where the time goes in v5:
time: 32.7 us; the launch traced here: 32.6 us
  Pallas kernels  31.2 us (95%)
  between operations  1.37 us (4%)
    pallas_call x1, Pallas kernels, sparse(): pl.pallas_call(functools.partial(swap_kernel, n), out_shape=jax.ShapeDtyp...  15 us
    pallas_call x1, Pallas kernels, sparse(): pl.pallas_call(functools.partial(send_kernel, n), out_shape=jax.ShapeDtyp...  8.8 us
    pallas_call x1, Pallas kernels, sparse(): pl.pallas_call(functools.partial(owner_kernel, n), out_shape=(jax.ShapeDt...  7.39 us

profile of v5, /device:TPU:0, one launch (start us, length us, event | category | flops | bytes accessed | tf_op | source)
XLA Modules:
  0.0 32.6 jit_solution(15699268193836383195)
XLA Ops:
  0.6 8.8 %shard_map.54.sent = s32[32,16,128]{2,1,0:T(8,128)S(1)} custom-call(s32[32,8,128]{2,1,0:T(8,128)} %bitcast.30, s32[32,8,128]{2,1,0:T(8,128)} %bitcast.31, f32[32,8,128]{2,1,0:T(8,128)} %bitcast.32), custom_call_target="tpu_custom_call" | custom-call | tf_op jit(solution)/shard_map/pallas_call | solution.py:441
  9.4 15.0 %shard_map.55.got_ref = s32[32,16,128]{2,1,0:T(8,128)S(1)} custom-call(s32[32,16,128]{2,1,0:T(8,128)S(1)} %shard_map.54.sent), custom_call_target="tpu_custom_call" | custom-call | tf_op jit(solution)/shard_map/pallas_call | solution.py:447
  24.4 7.4 %shard_map.56 = (f32[128,128]{1,0:T(8,128)}, s32[128,128]{1,0:T(8,128)}, s32[1]{0:T(128)}) custom-call(s32[32,16,128]{2,1,0:T(8,128)S(1)} %shard_map.55.got_ref), custom_call_target="tpu_custom_call" | custom-call | tf_op jit(solution)/shard_map/pallas_call | solution.py:458
  (1 shorter events, 0.0 us)

commit v6 on v5

--- a/solution.py
+++ b/solution.py
@@ -13,6 +13,7 @@
 EMPTY = (TOP + UNIT) * UNIT
 NONE = 1 << 30
 FAIL = -2000000000
+GAP = 1 << 19
 SUBS = 8
 LANES = 128
 GRANT = 16 << 20
@@ -212,44 +213,46 @@
     offset = run - column + scan - count
     for i in range(v):
         d = ds[i]
-        cs[i] = jnp.where(d < 0, NONE, cs[i])
-        ds[i] = jnp.where(d < 0, 0, d + offset)
-
-    def step(own, inc, bit):
-        c, k, d = own
-        pc, pk, pd = inc
-        comes = (pd & bit) != 0
-        goes = (d & bit) != 0
+        lost = d < 0
+        d = d + offset
+        cs[i] = jnp.where(lost, GAP, (d >> 4 << 20) | cs[i])
+        ks[i] = jnp.where(lost, 0, ((d & 15) << 27) | ks[i])
+
+    def step(own, inc, b):
+        c, k = own
+        pc, pk = inc
+        word, bit = (1, 1 << (27 + b)) if b < 4 else (0, 1 << (16 + b))
+        comes = (inc[word] & bit) != 0
+        goes = (own[word] & bit) != 0
         return (
-            jnp.where(comes, pc, jnp.where(goes, NONE, c)),
-            jnp.where(comes, pk, k),
-            jnp.where(comes, pd, jnp.where(goes, 0, d)),
+            jnp.where(comes, pc, jnp.where(goes, GAP, c)),
+            jnp.where(comes, pk, jnp.where(goes, 0, k)),
         )
 
-    now, then = (cs, ks, ds), (cs2, ks2, ds2)
+    now, then = (cs, ks), (cs2, ks2)
     for b in range(vbits):
         for i in range(v):
             j = i + (1 << b)
             own = tuple(r[i] for r in now)
             inc = tuple(r[j] if j < v else later(r[j - v], 1) for r in now)
-            for r, x in zip(then, step(own, inc, 1 << b)):
+            for r, x in zip(then, step(own, inc, b)):
                 r[i] = x
         now, then = then, now
-    for b in range(3):
+    for b in range(10):
         for i in range(v):
             own = tuple(r[i] for r in now)
-            inc = tuple(later(x, 1 << b) for x in own)
-            for r, x in zip(now, step(own, inc, 1 << (b + vbits))):
-                r[i] = x
-
-    for b in range(7):
-        shift = LANES - (1 << b)
-        for i in range(v):
-            own = tuple(r[i] for r in now)
-            inc = tuple(pltpu.roll(x, shift, 1) for x in own)
-            for r, x in zip(now, step(own, inc, 1 << (b + vbits + 3))):
-                r[i] = x
-    return now, then
+            if b < 3:
+                inc = tuple(later(x, 1 << b) for x in own)
+            else:
+                inc = tuple(pltpu.roll(x, LANES - (1 << (b - 3)), 1) for x in own)
+            c, k = step(own, inc, b + vbits)
+            if b == 9:
+                c = c & (2 * GAP - 1)
+                c = jnp.where(c == GAP, NONE, c)
+                k = k & ((1 << 27) - 1)
+            now[0][i] = c
+            now[1][i] = k
+    return now + (ds,), then + (ds2,)
 
 
 def expand(ks, ds, ks2, ds2):
@@ -367,8 +370,8 @@
     copies = []
     for k in sorted(range(1, n), key=lambda k: -(k % inner)):
         copy = pltpu.make_async_remote_copy(
-            src_ref=sent.at[me ^ k],
-            dst_ref=got.at[me],
+            src_ref=sent.at[me ^ k, 0 : 3 * ROWS],
+            dst_ref=got.at[me, 0 : 3 * ROWS],
             send_sem=send_sem.at[k],
             recv_sem=recv_sem.at[k],
             device_id=spot(me ^ k),

time: 32.7 us -> 31.7 us (0.969)
  Pallas kernels: 31.2 us -> 30.2 us
    pallas_call x1, Pallas kernels: 15 us -> 14.6 us  [sparse(): pl.pallas_call(functools.partial(swap_kernel, n), out_shape=jax.ShapeDtyp...]
    pallas_call x1, Pallas kernels: 7.39 us -> 7.06 us  [sparse(): pl.pallas_call(functools.partial(owner_kernel, n), out_shape=(jax.ShapeDt...]
where the time goes in v6:
time: 31.7 us; the launch traced here: 31.6 us
  Pallas kernels  30.2 us (95%)
  between operations  1.37 us (4%)
    pallas_call x1, Pallas kernels, sparse(): pl.pallas_call(functools.partial(swap_kernel, n), out_shape=jax.ShapeDtyp...  14.6 us
    pallas_call x1, Pallas kernels, sparse(): pl.pallas_call(functools.partial(send_kernel, n), out_shape=jax.ShapeDtyp...  8.5 us
    pallas_call x1, Pallas kernels, sparse(): pl.pallas_call(functools.partial(owner_kernel, n), out_shape=(jax.ShapeDt...  7.06 us

profile of v6, /device:TPU:0, one launch (start us, length us, event | category | flops | bytes accessed | tf_op | source)
XLA Modules:
  0.0 31.6 jit_solution(1960360678811976473)
XLA Ops:
  0.6 8.5 %shard_map.54.sent = s32[32,16,128]{2,1,0:T(8,128)S(1)} custom-call(s32[32,8,128]{2,1,0:T(8,128)} %bitcast.30, s32[32,8,128]{2,1,0:T(8,128)} %bitcast.31, f32[32,8,128]{2,1,0:T(8,128)} %bitcast.32), custom_call_target="tpu_custom_call" | custom-call | tf_op jit(solution)/shard_map/pallas_call | solution.py:444
  9.1 14.6 %shard_map.55.got_ref = s32[32,16,128]{2,1,0:T(8,128)S(1)} custom-call(s32[32,16,128]{2,1,0:T(8,128)S(1)} %shard_map.54.sent), custom_call_target="tpu_custom_call" | custom-call | tf_op jit(solution)/shard_map/pallas_call | solution.py:450
  23.8 7.1 %shard_map.56 = (f32[128,128]{1,0:T(8,128)}, s32[128,128]{1,0:T(8,128)}, s32[1]{0:T(128)}) custom-call(s32[32,16,128]{2,1,0:T(8,128)S(1)} %shard_map.55.got_ref), custom_call_target="tpu_custom_call" | custom-call | tf_op jit(solution)/shard_map/pallas_call | solution.py:461
  (1 shorter events, 0.0 us)
